TPU v7x, 16 devices: a whole 2x2x2 slice. The times are simulated.
16 devices in a mesh: dp: 4 (over z, y), ep: 4 (over x, core).
Axes of the slice: x: 2, y: 2, z: 2, core: 2. Of those that a mesh axis runs over, the one named last changes fastest.
Arguments:
- hidden_in: bfloat16 [4096, 2560], P(('dp', 'ep')), parts along dimension 0
- topk_idx: int32 [4096, 6], P(('dp', 'ep')), parts along dimension 0
- norm_gain: bfloat16 [2560], replicated
- w_router: bfloat16 [2560, 64], replicated
- w_sgate: bfloat16 [2560, 1], replicated
- s_gate: bfloat16 [2560, 3072], replicated
- s_up: bfloat16 [2560, 3072], replicated
- s_down: bfloat16 [3072, 2560], replicated
- w_gate: bfloat16 [64, 2560, 1536], P('ep')
- w_up: bfloat16 [64, 2560, 1536], P('ep')
- w_down: bfloat16 [64, 1536, 2560], P('ep')
Outputs:
- output: bfloat16 [4096, 2560], P(('dp', 'ep')), parts along dimension 0
There are 4 independent parts. A program takes and returns all parts, laid end to end along the dimension named above; an argument that names none is the same for every part.
All inputs are finite; a program needn't handle non-finite values.
Results may differ from a plain program's by a relative error of at most 0.001.
Values are sent between devices in bfloat16 or wider.
A program may use at most 1.75 GiB of HBM per device.

v0:
```python
import jax
import jax.numpy as jnp
from jax import lax
from jax.sharding import PartitionSpec as P


def rms_norm(hidden_in, norm_gain):
    x_f32 = hidden_in.astype(jnp.float32)
    inv_rms = lax.rsqrt(jnp.mean(x_f32 * x_f32, axis=-1, keepdims=True) + 1e-6)
    return (x_f32 * inv_rms * norm_gain.astype(jnp.float32)).astype(jnp.bfloat16)


def shared_expert(normed, w_sgate, s_gate, s_up, s_down):
    shared_act = (jax.nn.silu(jnp.dot(normed, s_gate, preferred_element_type=jnp.float32))
                  * jnp.dot(normed, s_up, preferred_element_type=jnp.float32)).astype(jnp.bfloat16)
    shared_val = jnp.dot(shared_act, s_down, preferred_element_type=jnp.float32)
    return jax.nn.sigmoid(jnp.dot(normed, w_sgate, preferred_element_type=jnp.float32)) * shared_val


def solution(mesh):
    group_size = mesh.shape['ep']

    def device_block(hidden_in, topk_idx, norm_gain, w_router, w_sgate, s_gate, s_up, s_down, w_gate, w_up, w_down):
        tok_dev, hidden = hidden_in.shape
        top_k = topk_idx.shape[1]
        experts = w_router.shape[1]
        slots_dev = w_gate.shape[0]
        num_slots = slots_dev * group_size
        capacity = (5 * tok_dev * group_size * top_k + 4 * experts - 1) // (4 * experts)
        local_max = (2 * tok_dev * top_k + experts - 1) // experts
        normed = rms_norm(hidden_in, norm_gain)
        router_probs = jax.nn.softmax(jnp.dot(normed, w_router, preferred_element_type=jnp.float32), axis=-1)
        gate_vals = jnp.take_along_axis(router_probs, topk_idx, axis=1)
        flat_ids = topk_idx.reshape(-1)
        onehot = (flat_ids[:, None] == jnp.arange(experts)[None, :]).astype(jnp.int32)
        local_pos = jnp.sum((jnp.cumsum(onehot, axis=0) - onehot) * onehot, axis=1)
        all_counts = lax.all_gather(jnp.sum(onehot, axis=0), 'ep')
        my_rank = lax.axis_index('ep')
        lower_counts = jnp.sum(jnp.where(jnp.arange(group_size)[:, None] < my_rank, all_counts, 0), axis=0)
        global_pos = jnp.take(lower_counts, flat_ids) + local_pos
        buf_pos = jnp.where(global_pos < capacity, flat_ids * local_max + local_pos, num_slots * local_max)
        token_of = jnp.arange(tok_dev * top_k) // top_k
        row_table = jnp.full((num_slots * local_max,), tok_dev, jnp.int32).at[buf_pos].set(token_of, mode='drop')
        send_buf = jnp.take(normed, row_table, axis=0, mode='fill', fill_value=0).reshape(num_slots, local_max, hidden)
        recv_buf = lax.all_to_all(send_buf, 'ep', 0, 1, tiled=True)
        gate_proj = jnp.einsum('sch,shf->scf', recv_buf, w_gate, preferred_element_type=jnp.float32)
        up_proj = jnp.einsum('sch,shf->scf', recv_buf, w_up, preferred_element_type=jnp.float32)
        expert_act = (jax.nn.silu(gate_proj) * up_proj).astype(jnp.bfloat16)
        expert_out = jnp.einsum('scf,sfh->sch', expert_act, w_down, preferred_element_type=jnp.float32).astype(jnp.bfloat16)
        back_buf = lax.all_to_all(expert_out, 'ep', 1, 0, tiled=True)
        picked = jnp.take(back_buf.reshape(num_slots * local_max, hidden), buf_pos, axis=0, mode='fill', fill_value=0)
        picked = picked.reshape(tok_dev, top_k, hidden)
        routed = jnp.sum(gate_vals[:, :, None] * picked.astype(jnp.float32), axis=1)
        shared_val = shared_expert(normed, w_sgate, s_gate, s_up, s_down)
        return (hidden_in.astype(jnp.float32) + routed + shared_val).astype(jnp.bfloat16)

    row_spec = P(('dp', 'ep'), None)
    full_spec = P(None, None)
    slot_spec = P('ep', None, None)
    in_specs = (row_spec, row_spec, P(None), full_spec, full_spec, full_spec, full_spec, full_spec,
                slot_spec, slot_spec, slot_spec)
    return jax.shard_map(device_block, mesh=mesh, in_specs=in_specs, out_specs=row_spec, check_vma=False)
```

profile of v0, /device:TPU:0, one launch (start us, length us, event | category | flops | bytes accessed | tf_op | source)
XLA Modules:
  0.0 747.6 jit_solution(5715964433772117034)
XLA Ops:
  0.0 0.9 copy.62
  1.2 18.1 %reduce-window.6 = s32[64,12,128]{2,1,0:T(8,128)S(1)} reduce-window(s32[64,12,128]{2,1,0:T(8,128)S(1)} %fusion.9, s32[]{:T(128)} %constant.50.clone.1), window={size=1x1x128 pad=0_0x0_0x127_0}, to_apply=%region_5.6 | reduce-window | flops 12484608 | bytes 786436 | tf_op jit(solution)/shard_map/reduce-window
  20.4 1.2 dynamic-slice
  22.5 6.6 all-reduce
  29.4 0.7 fusion.26
  30.9 0.7 fusion.24
  31.7 0.7 fusion.25
  32.4 4.3 fusion.18
  36.7 1.1 compare_reduce_fusion.56
  37.8 35.6 %select_select_fusion = s32[1536]{0:T(1024)S(1)} fusion(pred[1536]{0:T(1024)(128)(4,1)S(1)} %get-tuple-element.63, pred[1536]{0:T(1024)(128)(4,1)S(1)} %get-tuple-element.61, pred[1536]{0:T(1024)(128)(4,1)S(1)} %get-tuple-element.62, pred[1536]{0:T(1024)(128)(4,1)S(1)} %get-tuple-element.60, pred[1536]{0:T(1024)(128)(4,1)S(1)} %get-tuple-element.59, ...), kind=kLoop, calls=%fused_computation.113 | loop fusion | flops 87552 | bytes 100068 | tf_op jit(solution)/shard_map/jit(_take)/gather | solution.py:40
  74.1 6.2 scatter_custom_fusion
  80.4 0.7 convert_element_type.33
  81.1 1.7 fusion.6
  82.8 1.7 fusion.8
  84.5 16.8 %gather_fusion = bf16[3072,2560]{1,0:T(8,128)(2,1)} fusion(bf16[256,2560]{1,0:T(8,128)(2,1)S(1)} %fusion.8, s32[3072]{0:T(1024)S(1)} %fusion.14), kind=kCustom, calls=%fused_computation | custom fusion | bytes 31469568 | tf_op jit(solution)/shard_map/jit(_take)/gather | solution.py:44
  101.3 8.0 %broadcast_select_fusion = bf16[64,48,2560]{2,1,0:T(8,128)(2,1)S(1)} fusion(bf16[64,48,2560]{2,1,0:T(8,128)(2,1)} %bitcast.117, pred[64,48]{1,0:T(8,128)(4,1)S(1)} %broadcast_in_dim.74), kind=kLoop, calls=%fused_computation.6 | loop fusion | flops 7864320 | bytes 31460352 | tf_op jit(solution)/shard_map/jit(_take)/select_n | solution.py:44
  109.3 175.0 %all_to_all.33 = bf16[64,48,2560]{2,1,0:T(8,128)(2,1)S(1)} all-to-all(bf16[64,48,2560]{2,1,0:T(8,128)(2,1)S(1)} %broadcast_select_fusion), channel_id=1, replica_groups=mesh['dp'=4,'ep'=4] {'ep'}, dimensions={0} | all-to-all | bytes 31457280 | tf_op jit(solution)/shard_map/all_to_all | solution.py:45
  284.3 6.5 copy.71
  290.8 55.3 %fusion.29 = f32[16,192,1536]{2,1,0:T(8,128)} fusion(bf16[16,192,2560]{2,1,0:T(8,128)(2,1)} %bitcast.113, bf16[16,2560,1536]{2,1,0:T(8,128)(2,1)} %param.19), kind=kOutput, calls=%fused_computation.134 | convolution fusion | flops 24159191040 | bytes 160432128 | tf_op jit(solution)/shard_map/sch,shf->scf/dot_general | solution.py:46
  346.2 56.1 %multiply_convert_fusion.4 = bf16[16,192,1536]{2,1,0:T(8,128)(2,1)} fusion(f32[16,192,1536]{2,1,0:T(8,128)} %fusion.29, bf16[16,192,2560]{2,1,0:T(8,128)(2,1)} %bitcast.114, bf16[16,2560,1536]{2,1,0:T(8,128)(2,1)} %param.20), kind=kOutput, calls=%fused_computation.5.clone.clone.1 | convolution fusion | flops 24187502592 | bytes 169869312 | tf_op jit(solution)/shard_map/sch,shf->scf/dot_general | solution.py:47
  402.2 50.9 %convolution_convert_fusion = bf16[16,192,2560]{2,1,0:T(8,128)(2,1)} fusion(bf16[16,1536,2560]{2,1,0:T(8,128)(2,1)} %param.21, bf16[16,192,1536]{2,1,0:T(8,128)(2,1)} %multiply_convert_fusion.4), kind=kOutput, calls=%fused_computation.7 | convolution fusion | flops 24167055360 | bytes 150994944 | tf_op jit(solution)/shard_map/scf,sfh->sch/dot_general | solution.py:49
  453.2 23.4 %copy.72 = bf16[16,192,2560]{2,0,1:T(8,128)(2,1)} copy(bf16[16,192,2560]{2,1,0:T(8,128)(2,1)} %convolution_convert_fusion) | data formatting | bytes 31457280 | tf_op jit(solution)/shard_map/convert_element_type | solution.py:49
  476.6 7.0 all-to-all-start.1
  485.2 12.7 %gather_fusion.2 = f32[1536]{0:T(1024)S(1)} fusion(f32[256,64]{0,1:T(8,128)S(1)} %fusion.12, s32[1536]{0:T(1024)S(1)} %reshape.280), kind=kCustom, calls=%fused_computation.2 | custom fusion | bytes 24576 | tf_op jit(solution)/shard_map/jit(take_along_axis)/gather | solution.py:33
  498.8 7.7 %fusion.31 = f32[256,3072]{1,0:T(8,128)S(1)} fusion(bf16[256,2560]{1,0:T(8,128)(2,1)S(1)} %copy-done.2, bf16[2560,3072]{1,0:T(8,128)(2,1)} %param.16), kind=kOutput, calls=%fused_computation.136 | convolution fusion | flops 4026531840 | bytes 20185088 | tf_op jit(solution)/shard_map/dot_general | solution.py:14
  506.5 10.0 %fusion.5 = bf16[256,3072]{1,0:T(8,128)(2,1)S(1)} fusion(bf16[256,2560]{1,0:T(8,128)(2,1)S(1)} %copy-done.2, bf16[2560,3072]{1,0:T(8,128)(2,1)} %param.17, f32[256,3072]{1,0:T(8,128)S(1)} %fusion.31), kind=kOutput, calls=%fused_computation.17 | convolution fusion | flops 4031250432 | bytes 21757952 | tf_op jit(solution)/shard_map/dot_general | solution.py:15
  516.5 138.6 %all-to-all-done.1 = bf16[16,192,2560]{2,0,1:T(8,128)(2,1)} async-done(((bf16[16,192,2560]{2,0,1:T(8,128)(2,1)}), bf16[16,192,2560]{2,0,1:T(8,128)(2,1)}, u32[]{:S(2)}, u32[]{:S(2)}) %all-to-all-start.1) | async-done | bytes 15728672 | tf_op jit(solution)/shard_map/all_to_all | solution.py:50
  655.0 16.6 %copy.73 = bf16[16,4,48,2560]{3,2,0,1:T(8,128)(2,1)} copy(bf16[16,4,48,2560]{3,0,2,1:T(8,128)(2,1)} %bitcast.72) | data formatting | bytes 31457280 | tf_op jit(solution)/shard_map/all_to_all | solution.py:50
  671.7 22.9 %gather_fusion.1 = bf16[1536,2560]{1,0:T(8,128)(2,1)} fusion(bf16[3072,2560]{1,0:T(8,128)(2,1)} %bitcast.115, s32[2048]{0:T(1024)S(1)} %pad_clamp_fusion), kind=kCustom, calls=%fused_computation.1 | custom fusion | bytes 15734784 | tf_op jit(solution)/shard_map/jit(_take)/gather | solution.py:51
  694.5 13.0 %gather.31 = bf16[256,6,2560]{2,1,0:T(8,128)(2,1)} reshape(bf16[1536,2560]{1,0:T(8,128)(2,1)} %gather_fusion.1) | data formatting | bytes 15728640 | tf_op jit(solution)/shard_map/jit(_take)/gather | solution.py:51
  707.6 28.8 %multiply_reduce_fusion = f32[256,2560]{1,0:T(8,128)S(1)} fusion(bf16[256,6,2560]{2,1,0:T(8,128)(2,1)} %gather.31, f32[256,6]{1,0:T(8,128)S(1)} %copy.61, pred[256,6]{1,0:T(8,128)(4,1)S(1)} %copy.70), kind=kLoop, calls=%fused_computation.4 | loop fusion | flops 15073280 | bytes 10493440 | tf_op jit(solution)/shard_map/reduce_sum | solution.py:53
  736.4 10.8 %fusion.4 = bf16[256,2560]{1,0:T(8,128)(2,1)} fusion(bf16[256,3072]{1,0:T(8,128)(2,1)S(1)} %fusion.5, bf16[3072,2560]{1,0:T(8,128)(2,1)} %param.18, f32[256,2560]{1,0:T(8,128)S(1)} %multiply_reduce_fusion, bf16[256,2560]{1,0:T(8,128)(2,1)S(1)} %copy-done.3, f32[256]{0:T(256)S(1)} %add_divide_fusion), kind=kOutput, calls=%fused_computation.16 | convolution fusion | flops 4029808640 | bytes 22545408 | tf_op jit(solution)/shard_map/dot_general | solution.py:16
  (65 shorter events, 5.7 us)
Async XLA Ops:
  0.0 484.6 %copy-start = (bf16[2560,64]{0,1:T(8,128)(2,1)S(1)}, bf16[2560,64]{0,1:T(8,128)(2,1)}, u32[]{:S(2)}) copy-start(bf16[2560,64]{0,1:T(8,128)(2,1)} %param.14) | copy-start | bytes 983044
  20.4 53.1 %copy-start.5 = (s32[1536]{0:T(1024)}, s32[1536]{0:T(1024)S(1)}, u32[]{:S(2)}) copy-start(s32[1536]{0:T(1024)S(1)} %get-tuple-element.5) | copy-start | bytes 18436
  73.5 0.6 copy-start.7
  74.1 8.6 %copy-start.9 = (s32[1536]{0:T(1024)}, s32[1536]{0:T(1024)S(1)}, u32[]{:S(2)}) copy-start(s32[1536]{0:T(1024)S(1)} %fusion.19) | copy-start | bytes 18436
  84.5 16.8 %copy-start.1 = (bf16[256,2560]{1,0:T(8,128)(2,1)}, bf16[256,2560]{1,0:T(8,128)(2,1)S(1)}, u32[]{:S(2)}) copy-start(bf16[256,2560]{1,0:T(8,128)(2,1)S(1)} %fusion.8) | copy-start | bytes 3932164
  476.6 7.0 copy-start.8
  476.6 7.1 copy-start.6
  476.6 7.4 copy-start.4
  476.6 8.0 %copy-start.2 = (bf16[256,2560]{1,0:T(8,128)(2,1)S(1)}, bf16[256,2560]{1,0:T(8,128)(2,1)}, u32[]{:S(2)}) copy-start(bf16[256,2560]{1,0:T(8,128)(2,1)} %copy-done.1) | copy-start | bytes 3932164
  476.6 178.4 %all-to-all-start.1 = ((bf16[16,192,2560]{2,0,1:T(8,128)(2,1)}), bf16[16,192,2560]{2,0,1:T(8,128)(2,1)}, u32[]{:S(2)}, u32[]{:S(2)}) async-start(bf16[16,192,2560]{2,0,1:T(8,128)(2,1)} %copy.72), calls=%async_computation.1 | async-start | bytes 31457280 | tf_op jit(solution)/shard_map/all_to_all | solution.py:50
  485.2 13.1 %copy-start.10 = (s32[1536]{0:T(1024)S(1)}, s32[1536]{0:T(1024)}, u32[]{:S(2)}) copy-start(s32[1536]{0:T(1024)} %copy-done.9) | copy-start | bytes 18436
  485.2 13.2 %copy-start.11 = (bf16[2560,1]{0,1:T(2,128)(2,1)S(1)}, bf16[2560,1]{0,1:T(2,128)(2,1)}, u32[]{:S(2)}) copy-start(bf16[2560,1]{0,1:T(2,128)(2,1)} %param.15) | copy-start | bytes 15364
  707.6 28.8 %copy-start.3 = (bf16[256,2560]{1,0:T(8,128)(2,1)S(1)}, bf16[256,2560]{1,0:T(8,128)(2,1)}, u32[]{:S(2)}) copy-start(bf16[256,2560]{1,0:T(8,128)(2,1)} %param.11) | copy-start | bytes 3932164
where the time goes:
time: 754 us; the launch traced here: 748 us
  matrix products  192 us (25%)
  blocking collectives  182 us (24%)
  waiting for transfers between devices  139 us (18%)
  local copies, waits for them, and re-layouts  126 us (17%)
  other arithmetic  101 us (13%)
    all_to_all x1, blocking collectives, device_block(): recv_buf = lax.all_to_all(send_buf, 'ep', 0, 1, tiled=True)  175 us
    all_to_all x1, waiting for transfers between devices, device_block(): back_buf = lax.all_to_all(expert_out, 'ep', 1, 0, tiled=True)  139 us
    dot_general x1, matrix products, device_block(): jnp.einsum('sch,shf->scf', recv_buf, w_up, preferred_element_type=jnp.flo...  56.1 us
    dot_general x1, matrix products, device_block(): jnp.einsum('sch,shf->scf', recv_buf, w_gate, preferred_element_type=jnp.f...  55.3 us
    dot_general x1, matrix products, device_block(): jnp.einsum('scf,sfh->sch', expert_act, w_down, preferred_element_type=jnp...  50.9 us
    gather x3, other arithmetic, device_block(): global_pos = jnp.take(lower_counts, flat_ids) + local_pos  41.1 us
    gather x2, local copies, waits for them, and re-layouts, device_block(): jnp.take(back_buf.reshape(num_slots * local_max, hidden), buf_pos, axis=0...  35.9 us
    reduce_sum x1, other arithmetic, device_block(): routed = jnp.sum(gate_vals[:, :, None] * picked.astype(jnp.float32), axis=1)  28.8 us
  transfers between devices with their start and end apart: 1, of which 1 were waited for; matrix products, arithmetic and copies ran while one was open for 4% of the time, Pallas kernels for 0%

commit v1 on v0

v1 whole, which is shorter than its diff:
```python
import functools

import jax
import jax.numpy as jnp
from jax import lax
from jax.experimental import pallas as pl
from jax.experimental.pallas import tpu as pltpu
from jax.sharding import PartitionSpec as P

F32 = jnp.float32
BF16 = jnp.bfloat16
LANES = 128


def rms_norm(hidden_in, norm_gain):
    x_f32 = hidden_in.astype(F32)
    inv_rms = lax.rsqrt(jnp.mean(x_f32 * x_f32, axis=-1, keepdims=True) + 1e-6)
    return (x_f32 * inv_rms * norm_gain.astype(F32)).astype(BF16)


def shared_expert(normed, w_sgate, s_gate, s_up, s_down):
    shared_act = (jax.nn.silu(jnp.dot(normed, s_gate, preferred_element_type=F32))
                  * jnp.dot(normed, s_up, preferred_element_type=F32)).astype(BF16)
    shared_val = jnp.dot(shared_act, s_down, preferred_element_type=F32)
    return jax.nn.sigmoid(jnp.dot(normed, w_sgate, preferred_element_type=F32)) * shared_val


def kept_positions(idx, lower, capacity):
    tok = idx.shape[0]
    lane = lax.broadcasted_iota(jnp.int32, (tok, LANES), 1)
    hit = lane == idx[:, 0:1]
    for k in range(1, idx.shape[1]):
        hit = jnp.logical_or(hit, lane == idx[:, k:k + 1])
    chosen = jnp.where(hit, 1.0, 0.0).astype(F32)
    row = lax.broadcasted_iota(jnp.int32, (tok, tok), 0)
    col = lax.broadcasted_iota(jnp.int32, (tok, tok), 1)
    below = jnp.where(col < row, 1.0, 0.0).astype(BF16)
    pos = jnp.dot(below, chosen.astype(BF16), preferred_element_type=F32)
    kept = jnp.logical_and(hit, pos + lower < capacity)
    return jnp.where(kept, pos, -1.0), lower + jnp.sum(chosen, axis=0, keepdims=True)


def gate_up_kernel(group, slots, local_max, capacity, h_ref, idx_ref, wg_ref, wu_ref, act_ref, pos_ref, x_ref, post_ref, pick_ref):
    expert, part = pl.program_id(0), pl.program_id(1)
    tok = idx_ref.shape[0] // group
    hidden = h_ref.shape[1]
    me = lax.axis_index('ep')

    @pl.when(jnp.logical_and(expert == 0, part == 0))
    def _():
        lower = jnp.zeros((1, LANES), F32)
        for src in range(group):
            pos, lower = kept_positions(idx_ref[src * tok:(src + 1) * tok, :], lower, capacity)
            pos_ref[src * tok:(src + 1) * tok, :] = pos
            post_ref[...] = jnp.transpose(pos)
            n_iota = lax.broadcasted_iota(jnp.int32, (local_max, tok), 0).astype(F32)
            for slot in range(slots):
                row = post_ref[pl.ds(me * slots + slot, 1), :]
                pick_ref[slot * local_max:(slot + 1) * local_max, :] = jnp.where(n_iota == row, 1.0, 0.0).astype(BF16)

            @pl.loop(0, hidden // 256)
            def _(c):
                cols = pl.ds(pl.multiple_of(c * 256, 256), 256)
                rows = jnp.dot(pick_ref[...], h_ref[src * tok:(src + 1) * tok, cols], preferred_element_type=F32)
                x_ref[:, src * local_max:(src + 1) * local_max, cols] = rows.astype(BF16).reshape(slots, local_max, 256)

    rows = x_ref[expert]
    gate = jnp.dot(rows, wg_ref[0], preferred_element_type=F32)
    up = jnp.dot(rows, wu_ref[0], preferred_element_type=F32)
    act_ref[0] = (jax.nn.silu(gate) * up).astype(BF16)


def gate_up(h_all, idx_all, w_gate, w_up, group, capacity, local_max, block=512):
    slots, hidden, ff = w_gate.shape
    tokens = h_all.shape[0]
    tok = tokens // group
    rows = group * local_max
    whole = lambda shape: pl.BlockSpec(shape, lambda e, j: (0,) * len(shape), pipeline_mode=pl.Buffered(1))
    w_spec = pl.BlockSpec((1, hidden, block), lambda e, j: (e, 0, j))
    return pl.pallas_call(
        functools.partial(gate_up_kernel, group, slots, local_max, capacity),
        out_shape=(jax.ShapeDtypeStruct((slots, rows, ff), BF16), jax.ShapeDtypeStruct((tokens, LANES), F32)),
        grid=(slots, ff // block),
        in_specs=[whole((tokens, hidden)), whole(idx_all.shape), w_spec, w_spec],
        out_specs=(pl.BlockSpec((1, rows, block), lambda e, j: (e, 0, j)), pl.BlockSpec((tokens, LANES), lambda e, j: (0, 0))),
        scratch_shapes=[pltpu.VMEM((slots, rows, hidden), BF16), pltpu.VMEM((LANES, tok), F32), pltpu.VMEM((slots * local_max, tok), BF16)],
        compiler_params=pltpu.CompilerParams(vmem_limit_bytes=60 << 20, dimension_semantics=("arbitrary", "arbitrary")),
        cost_estimate=pl.CostEstimate(flops=4 * slots * rows * hidden * ff, bytes_accessed=4 * slots * hidden * ff, transcendentals=0),
        name="gate_up",
    )(h_all, idx_all, w_gate, w_up)


def split3(value):
    high = value.astype(BF16)
    rest = value - high.astype(F32)
    mid = rest.astype(BF16)
    return high, mid, (rest - mid.astype(F32)).astype(BF16)


def combine_weights(pos, prob, me, slots, local_max):
    width = slots * local_max
    slot_of = lax.shift_right_logical(lax.broadcasted_iota(jnp.int32, (LANES, width), 1) * (65536 // local_max + 1), 16)
    spread = jnp.where(lax.broadcasted_iota(jnp.int32, (LANES, width), 0) == slot_of + me * slots, 1.0, 0.0).astype(BF16)
    col = lax.broadcasted_iota(jnp.int32, (pos.shape[0], width), 1)
    place = (col - lax.shift_right_logical(col * (65536 // local_max + 1), 16) * local_max).astype(F32)
    here = jnp.dot(pos.astype(BF16), spread, preferred_element_type=F32) == place
    return [jnp.where(here, jnp.dot(piece, spread, preferred_element_type=F32), 0.0).astype(BF16) for piece in split3(prob)]


def down_kernel(group, slots, local_max, per, act_ref, pos_ref, prob_ref, wd_ref, y_ref, comb_ref, out_ref):
    chunk, step = pl.program_id(0), pl.program_id(1)
    tok = pos_ref.shape[0] // group
    me = lax.axis_index('ep')

    @pl.when(jnp.logical_and(chunk == 0, step == 0))
    def _():
        for dst in range(group):
            rows = slice(dst * tok, (dst + 1) * tok)
            for i, piece in enumerate(combine_weights(pos_ref[rows, :], prob_ref[rows, :], me, slots, local_max)):
                comb_ref[dst, i * tok:(i + 1) * tok, :] = piece

    for i in range(per):
        res = jnp.dot(act_ref[step * per + i], wd_ref[i], preferred_element_type=F32).astype(BF16)
        at = pl.ds(pl.multiple_of((step * per + i) * local_max, local_max), local_max)
        for dst in range(group):
            out_ref[dst, at, :] = res[dst * local_max:(dst + 1) * local_max, :]

    @pl.when(step == pl.num_programs(1) - 1)
    def _():
        for dst in range(group):
            part = jnp.dot(comb_ref[dst], out_ref[dst], preferred_element_type=F32)
            y_ref[dst] = part[:tok] + part[tok:2 * tok] + part[2 * tok:]


def down(act, pos_all, prob_all, w_down, group, local_max, block=512, per=4):
    slots, ff, hidden = w_down.shape
    rows = act.shape[1]
    tokens = pos_all.shape[0]
    tok = tokens // group
    whole = lambda shape: pl.BlockSpec(shape, lambda j, e: (0,) * len(shape), pipeline_mode=pl.Buffered(1))
    return pl.pallas_call(
        functools.partial(down_kernel, group, slots, local_max, per),
        out_shape=jax.ShapeDtypeStruct((group, tok, hidden), F32),
        grid=(hidden // block, slots // per),
        in_specs=[whole(act.shape), whole(pos_all.shape), whole(prob_all.shape),
                  pl.BlockSpec((per, ff, block), lambda j, e: (e, 0, j))],
        out_specs=pl.BlockSpec((group, tok, block), lambda j, e: (0, 0, j)),
        scratch_shapes=[pltpu.VMEM((group, 3 * tok, slots * local_max), BF16), pltpu.VMEM((group, slots * local_max, block), BF16)],
        compiler_params=pltpu.CompilerParams(vmem_limit_bytes=60 << 20, dimension_semantics=("arbitrary", "arbitrary")),
        cost_estimate=pl.CostEstimate(flops=4 * slots * rows * hidden * ff // 2, bytes_accessed=2 * slots * hidden * ff, transcendentals=0),
        name="down",
    )(act, pos_all, prob_all, w_down)


def solution(mesh):
    group = mesh.shape['ep']

    def device_block(hidden_in, topk_idx, norm_gain, w_router, w_sgate, s_gate, s_up, s_down, w_gate, w_up, w_down):
        tok_dev, hidden = hidden_in.shape
        top_k = topk_idx.shape[1]
        experts = w_router.shape[1]
        capacity = (5 * tok_dev * group * top_k + 4 * experts - 1) // (4 * experts)
        local_max = (2 * tok_dev * top_k + experts - 1) // experts
        normed = rms_norm(hidden_in, norm_gain)
        probs = jax.nn.softmax(jnp.dot(normed, w_router, preferred_element_type=F32), axis=-1)
        probs = jnp.pad(probs, ((0, 0), (0, LANES - experts)))
        h_all = lax.all_gather(normed, 'ep', tiled=True)
        idx_all = lax.all_gather(topk_idx, 'ep', tiled=True)
        prob_all = lax.all_gather(probs, 'ep', tiled=True)
        shared_val = shared_expert(normed, w_sgate, s_gate, s_up, s_down)
        act, pos_all = gate_up(h_all, idx_all, w_gate, w_up, group, capacity, local_max)
        parts = down(act, pos_all, prob_all, w_down, group, local_max)
        routed = lax.psum_scatter(parts.reshape(group * tok_dev, hidden), 'ep', tiled=True)
        return (hidden_in.astype(F32) + routed + shared_val).astype(BF16)

    row_spec = P(('dp', 'ep'), None)
    full_spec = P(None, None)
    slot_spec = P('ep', None, None)
    in_specs = (row_spec, row_spec, P(None), full_spec, full_spec, full_spec, full_spec, full_spec,
                slot_spec, slot_spec, slot_spec)
    return jax.shard_map(device_block, mesh=mesh, in_specs=in_specs, out_specs=row_spec, check_vma=False)
```

time: 754 us -> 335 us (0.44)
  Pallas kernels: 0 us -> 179 us
  blocking collectives: 182 us -> 19.4 us
  matrix products: 192 us -> 33.4 us
  local copies, waits for them, and re-layouts: 126 us -> 1.55 us
  other arithmetic: 101 us -> 5.5 us
  waiting for transfers between devices: 139 us -> 81.4 us
  between operations: 1.49 us -> 13.5 us
    pallas_call x0 -> x2, Pallas kernels: none -> 179 us  [the longest x1 112 us: gate_up(): pl.pallas_call(functools.partial(gate_up_kernel, group, slots, local_max,...]
    all_to_all x1 -> x0, blocking collectives: 175 us -> none  [device_block(): recv_buf = lax.all_to_all(send_buf, 'ep', 0, 1, tiled=True)]
    dot_general x8 -> x5, matrix products: 192 us -> 33.4 us  [the longest x1 12 us: shared_expert(): shared_val = jnp.dot(shared_act, s_down, preferred_element_type=F32)]
    all_to_all x1 -> x0, waiting for transfers between devices: 139 us -> none  [device_block(): back_buf = lax.all_to_all(expert_out, 'ep', 1, 0, tiled=True)]
    gather x14 -> x0, local copies, waits for them, and re-layouts: 69 us -> none  [the longest x2 35.9 us: device_block(): jnp.take(back_buf.reshape(num_slots * local_max, hidden), buf_pos, axis=0...]
    reduce_scatter x0 -> x1, waiting for transfers between devices: none -> 59 us  [device_block(): lax.psum_scatter(parts.reshape(group * tok_dev, hidden), 'ep', tiled=True)]
    gather x6 -> x0, other arithmetic: 41.1 us -> none  [the longest x3 41.1 us: device_block(): global_pos = jnp.take(lower_counts, flat_ids) + local_pos]
    reduce_sum x4 -> x1, other arithmetic: 29.2 us -> 0.19 us  [device_block(): jax.nn.softmax(jnp.dot(normed, w_router, preferred_element_type=F32), axi...]
  transfers between devices with their start and end apart: 1 -> 2, of which waited for: 1 -> 2; matrix products, arithmetic and copies ran while one was open for 4% -> 7% of each run, Pallas kernels for 0% -> 0%
where the time goes in v1:
time: 335 us; the launch traced here: 334 us
  Pallas kernels  179 us (53%)
  waiting for transfers between devices  81.4 us (24%)
  matrix products  33.4 us (10%)
  blocking collectives  19.4 us (6%)
  between operations  13.5 us (4%)
  other arithmetic  5.5 us (2%)
    pallas_call x1, Pallas kernels, gate_up(): pl.pallas_call(functools.partial(gate_up_kernel, group, slots, local_max,...  112 us
    pallas_call x1, Pallas kernels, down(): pl.pallas_call(functools.partial(down_kernel, group, slots, local_max, pe...  67 us
    reduce_scatter x1, waiting for transfers between devices, device_block(): lax.psum_scatter(parts.reshape(group * tok_dev, hidden), 'ep', tiled=True)  59 us
    all_gather x1, waiting for transfers between devices, device_block(): h_all = lax.all_gather(normed, 'ep', tiled=True)  22.3 us
    dot_general x1, matrix products, shared_expert(): shared_val = jnp.dot(shared_act, s_down, preferred_element_type=F32)  12 us
    dot_general x1, matrix products, shared_expert(): jnp.dot(normed, s_up, preferred_element_type=F32)  11.4 us
    all_gather x1, blocking collectives, device_block(): prob_all = lax.all_gather(probs, 'ep', tiled=True)  10.5 us
    all_gather x1, blocking collectives, device_block(): idx_all = lax.all_gather(topk_idx, 'ep', tiled=True)  8.93 us
  transfers between devices with their start and end apart: 2, of which 2 were waited for; matrix products, arithmetic and copies ran while one was open for 7% of the time, Pallas kernels for 0%

profile of v1, /device:TPU:0, one launch (start us, length us, event | category | flops | bytes accessed | tf_op | source)
XLA Modules:
  0.0 334.1 jit_solution(681760705875659153)
XLA Ops:
  6.5 0.0 copy-start
  6.5 0.0 all-gather.2.cloned.1.call-start
  6.5 0.7 convert_element_type.19
  7.3 1.7 fusion.3
  8.9 0.0 copy-start.5
  9.0 2.8 fusion.5
  11.7 0.0 all-gather.2.cloned.1.call-update
  11.7 0.0 reduce-scatter.2.cloned.1.call-start
  11.8 0.0 copy-done
  11.8 1.8 fusion.8
  13.6 0.1 copy.13
  13.7 0.0 copy-done.5
  13.7 0.1 copy.12
  13.9 0.2 fusion.7
  14.1 0.1 fusion.6
  14.3 8.9 %all_gather.10.idx_ref = s32[1024,6]{1,0:T(8,128)} all-gather(s32[256,6]{1,0:T(8,128)S(1)} %copy.12), channel_id=1, replica_groups=mesh['dp'=4,'ep'=4] {'ep'}, dimensions={0}, use_global_device_ids=true | all-gather | bytes 30720 | tf_op jit(solution)/shard_map/all_gather | solution.py:168
  23.2 10.5 %all_gather.11.prob_ref = f32[1024,128]{1,0:T(8,128)} all-gather(f32[256,128]{1,0:T(8,128)S(1)} %pad.4), channel_id=1, replica_groups=mesh['dp'=4,'ep'=4] {'ep'}, dimensions={0}, use_global_device_ids=true | all-gather | bytes 655360 | tf_op jit(solution)/shard_map/all_gather | solution.py:169
  33.7 22.3 %all-gather.2.cloned.1.call-done.h_ref = bf16[1024,2560]{1,0:T(8,128)(2,1)} async-done(((bf16[256,2560]{1,0:T(8,128)(2,1)}), bf16[1024,2560]{1,0:T(8,128)(2,1)}) %all-gather.2.cloned.1.call-update) | async-done | bytes 5242896 | tf_op jit(solution)/shard_map/all_gather | solution.py:167
  56.0 112.4 %gate_up.1 = (bf16[16,192,1536]{2,1,0:T(8,128)(2,1)}, f32[1024,128]{1,0:T(8,128)}) custom-call(bf16[1024,2560]{1,0:T(8,128)(2,1)} %all-gather.2.cloned.1.call-done.h_ref, s32[1024,6]{1,0:T(8,128)} %all_gather.10.idx_ref, bf16[16,2560,1536]{2,1,0:T(8,128)(2,1)} %wg_ref.1, bf16[16,2560,1536]{2,1,0:T(8,128)(2,1)} %wu_ref.1), custom_call_target="tpu_custom_call" | custom-call | flops 48318382080 | bytes 251658240 | tf_op jit(solution)/shard_map/gate_up/pallas_call | solution.py:80
  168.4 67.0 %down.1 = f32[4,256,2560]{2,1,0:T(8,128)} custom-call(bf16[16,192,1536]{2,1,0:T(8,128)(2,1)} %get-tuple-element.7.act_ref, f32[1024,128]{1,0:T(8,128)} %get-tuple-element.8.pos_ref, f32[1024,128]{1,0:T(8,128)} %all_gather.11.prob_ref, bf16[16,1536,2560]{2,1,0:T(8,128)(2,1)} %wd_ref.1), custom_call_target="tpu_custom_call" | custom-call | flops 24159191040 | bytes 125829120 | tf_op jit(solution)/shard_map/down/pallas_call | solution.py:141
  235.4 0.0 copy-start.2
  235.4 0.0 reduce-scatter.2.cloned.1.call-update
  235.4 1.3 copy-done.2
  236.7 0.0 copy-done.4
  236.7 0.4 fusion.9
  237.1 7.7 %fusion.10 = f32[256,3072]{1,0:T(8,128)S(1)} fusion(bf16[256,2560]{1,0:T(8,128)(2,1)S(1)} %copy-done.2, bf16[2560,3072]{1,0:T(8,128)(2,1)} %param.16), kind=kOutput, calls=%fused_computation.18 | convolution fusion | flops 4026531840 | bytes 20185088 | tf_op jit(solution)/shard_map/dot_general | solution.py:22
  244.9 0.0 copy-start.3
  244.9 11.4 %fusion.2 = bf16[256,3072]{1,0:T(8,128)(2,1)} fusion(bf16[256,2560]{1,0:T(8,128)(2,1)S(1)} %copy-done.2, bf16[2560,3072]{1,0:T(8,128)(2,1)} %param.17, f32[256,3072]{1,0:T(8,128)S(1)} %fusion.10), kind=kOutput, calls=%fused_computation.7 | convolution fusion | flops 4031250432 | bytes 21757952 | tf_op jit(solution)/shard_map/dot_general | solution.py:23
  256.2 59.0 %reduce-scatter.2.cloned.1.call-done = f32[256,2560]{1,0:T(8,128)} async-done(((f32[1024,2560]{1,0:T(8,128)}), f32[256,2560]{1,0:T(8,128)}) %reduce-scatter.2.cloned.1.call-update) | async-done | bytes 2621456 | tf_op jit(solution)/shard_map/reduce_scatter | solution.py:173
  315.2 0.0 copy-done.3
  315.2 12.0 %fusion.1 = bf16[256,2560]{1,0:T(8,128)(2,1)} fusion(bf16[256,3072]{1,0:T(8,128)(2,1)} %fusion.2, bf16[3072,2560]{1,0:T(8,128)(2,1)} %param.18, f32[256,2560]{1,0:T(8,128)} %reduce-scatter.2.cloned.1.call-done, bf16[256,2560]{1,0:T(8,128)(2,1)S(1)} %copy-done.3, f32[256]{0:T(256)S(1)} %add_divide_fusion), kind=kOutput, calls=%fused_computation.6 | convolution fusion | flops 4029808640 | bytes 22545408 | tf_op jit(solution)/shard_map/dot_general | solution.py:24
  327.3 0.0 copy-done.1
  (5 shorter events, 0.0 us)
Async XLA Ops:
  6.5 5.2 %copy-start = (bf16[2560,64]{0,1:T(8,128)(2,1)S(1)}, bf16[2560,64]{0,1:T(8,128)(2,1)}, u32[]{:S(2)}) copy-start(bf16[2560,64]{0,1:T(8,128)(2,1)} %param.14) | copy-start | bytes 983044
  6.5 49.4 %all-gather.2.cloned.1.call-start = ((), (), s32[]{:S(2)}) async-start(), calls=%async_computation.1 | async-start | bytes 6553600 | tf_op jit(solution)/shard_map/all_gather | solution.py:167
  8.9 4.8 %copy-start.5 = (s32[256,6]{0,1:T(8,128)S(1)}, s32[256,6]{0,1:T(8,128)}, u32[]{:S(2)}) copy-start(s32[256,6]{0,1:T(8,128)} %param.12) | copy-start | bytes 18436
  11.7 303.5 %reduce-scatter.2.cloned.1.call-start = ((), (), s32[]{:S(2)}) async-start(), calls=%async_computation.2 | async-start | bytes 13107200 | tf_op jit(solution)/shard_map/reduce_scatter | solution.py:173
  235.4 1.3 copy-start.2
  235.4 1.3 copy-start.4
  244.9 70.4 %copy-start.3 = (bf16[256,2560]{1,0:T(8,128)(2,1)S(1)}, bf16[256,2560]{1,0:T(8,128)(2,1)}, u32[]{:S(2)}) copy-start(bf16[256,2560]{1,0:T(8,128)(2,1)} %param.11) | copy-start | bytes 3932164
  315.2 12.0 %copy-start.1 = (bf16[2560,64]{0,1:T(8,128)(2,1)S(1)}, bf16[2560,64]{0,1:T(8,128)(2,1)}, u32[]{:S(2)}) copy-start(bf16[2560,64]{0,1:T(8,128)(2,1)} %param.14) | copy-start | bytes 983044
Sparse Core Ops, SparseCore 0:
  11.9 44.0 all-gather.1
  235.5 79.6 reduce-scatter.1

commit v2 on v0

v2 whole, which is shorter than its diff:
```python
import functools

import jax
import jax.numpy as jnp
from jax import lax
from jax.experimental import pallas as pl
from jax.experimental.pallas import tpu as pltpu
from jax.sharding import PartitionSpec as P

F32 = jnp.float32
BF16 = jnp.bfloat16
MESH = pl.DeviceIdType.MESH
DEPTH = 4
WIDTH = 512
PIECES = 4


def aligned(start, size):
    return pl.ds(pl.multiple_of(start, size), size)


def moe_kernel(group, experts, capacity, local_max,
               x_hbm, idx_ref, gain_ref, wr_hbm, wsg_ref, sg_hbm, su_hbm, sd_hbm, wg_hbm, wu_hbm, wd_hbm,
               out_hbm,
               ring, xbuf, act, hbuf, pair, relay, fromsib, fromchip, acc, prob, post, sgate, idx_all, wr, counts,
               ring_sem, in_sem, out_sem, idx_send, idx_recv, h_send, h_recv, sib_send, sib_recv, fwd_send, fwd_recv,
               p_send, p_recv, pair_send, pair_recv, relay_send, relay_recv, credit):
    tok, hidden = x_hbm.shape
    slots, _, ff = wg_hbm.shape
    top_k = idx_ref.shape[0]
    rows = group * local_max
    width = slots * local_max
    n_s1 = 2 * ff // WIDTH
    n_s2 = hidden // WIDTH
    parts = ff // WIDTH
    n_g = slots * parts
    n_chunk = hidden // WIDTH
    n_pair = slots // 2
    n_d = n_chunk * n_pair
    first_g, first_d = n_s1 + n_s2, n_s1 + n_s2 + n_g
    total = first_d + n_d
    piece = tok // PIECES

    me = lax.axis_index('ep')
    sib = me + 1 - 2 * lax.rem(me, 2)
    far = lax.rem(me + 2, group)
    diag = lax.rem(sib + 2, group)

    def shared_up(n, s):
        cols = aligned(n * WIDTH, WIDTH)
        return (pltpu.make_async_copy(sg_hbm.at[:, cols], ring.at[s, 0], ring_sem.at[s, 0]),
                pltpu.make_async_copy(su_hbm.at[:, cols], ring.at[s, 1], ring_sem.at[s, 1]))

    def shared_down(n, s):
        cols = aligned(n * WIDTH, WIDTH)
        return tuple(pltpu.make_async_copy(sd_hbm.at[i * ff:(i + 1) * ff, cols], ring.at[s, i, 0:ff, :], ring_sem.at[s, i])
                     for i in range(2))

    def expert_up(n, s):
        e, cols = n // parts, aligned(lax.rem(n, parts) * WIDTH, WIDTH)
        return (pltpu.make_async_copy(wg_hbm.at[e, :, cols], ring.at[s, 0], ring_sem.at[s, 0]),
                pltpu.make_async_copy(wu_hbm.at[e, :, cols], ring.at[s, 1], ring_sem.at[s, 1]))

    def expert_down(n, s):
        e, cols = lax.rem(n, n_pair) * 2, aligned(n // n_pair * WIDTH, WIDTH)
        return tuple(pltpu.make_async_copy(wd_hbm.at[e + i, :, cols], ring.at[s, i, 0:ff, :], ring_sem.at[s, i])
                     for i in range(2))

    def start(copies):
        for copy in copies:
            copy.start()

    def wait(copies):
        for copy in copies:
            copy.wait()

    def issue(n):
        s = lax.rem(n, DEPTH)

        @pl.when(n < n_s1)
        def _():
            start(shared_up(n, s))

        @pl.when(jnp.logical_and(n >= n_s1, n < first_g))
        def _():
            start(shared_down(n - n_s1, s))

        @pl.when(jnp.logical_and(n >= first_g, n < first_d))
        def _():
            start(expert_up(n - first_g, s))

        @pl.when(jnp.logical_and(n >= first_d, n < total))
        def _():
            start(expert_down(n - first_d, s))

    def remote(src, dst, send, recv, to):
        return pltpu.make_async_remote_copy(src_ref=src, dst_ref=dst, send_sem=send, recv_sem=recv,
                                            device_id={'ep': to}, device_id_type=MESH)

    def h_piece(owner, i):
        return hbuf.at[owner, i * piece:(i + 1) * piece, :]

    def send_h(i):
        return remote(h_piece(me, i), h_piece(me, i), h_send.at[i], h_recv.at[i], far)

    def take_h(i):
        return remote(h_piece(far, i), h_piece(far, i), h_send.at[i], h_recv.at[i], far)

    def send_sib():
        return remote(hbuf.at[me], hbuf.at[me], sib_send, sib_recv, sib)

    def take_sib():
        return remote(hbuf.at[sib], hbuf.at[sib], sib_send, sib_recv, sib)

    def pass_h(i):
        return remote(h_piece(far, i), h_piece(far, i), fwd_send.at[i], fwd_recv.at[i], sib)

    def take_passed(i):
        return remote(h_piece(diag, i), h_piece(diag, i), fwd_send.at[i], fwd_recv.at[i], sib)

    def three(buf, send, recv):
        mine = [remote(buf.at[me], buf.at[me], send.at[0], recv.at[0], far),
                remote(buf.at[me], buf.at[me], send.at[1], recv.at[1], sib),
                remote(buf.at[far], buf.at[far], send.at[2], recv.at[2], sib)]
        theirs = [remote(buf.at[far], buf.at[far], send.at[0], recv.at[0], far),
                  remote(buf.at[sib], buf.at[sib], send.at[1], recv.at[1], sib),
                  remote(buf.at[diag], buf.at[diag], send.at[2], recv.at[2], sib)]
        return mine, theirs

    idx_out, idx_in = three(idx_all, idx_send, idx_recv)
    p_out, p_in = three(prob, p_send, p_recv)

    load_x = pltpu.make_async_copy(x_hbm, hbuf.at[me], in_sem.at[0])
    load_x.start()
    load_r = pltpu.make_async_copy(wr_hbm, wr, in_sem.at[1])
    load_r.start()
    barrier = pltpu.get_barrier_semaphore()
    for peer in (sib, far):
        pl.semaphore_signal(barrier, inc=1, device_id={'ep': peer}, device_id_type=MESH)
    idx_all[me] = idx_ref[...]
    load_x.wait()
    start(shared_up(0, 0))
    start(shared_up(1, 1))
    pl.semaphore_wait(barrier, 2)
    idx_out[0].start()
    idx_out[1].start()

    gain = gain_ref[...].astype(F32).reshape(1, hidden)
    for i in range(PIECES):
        @pl.loop(0, piece // 32)
        def _(b):
            at = aligned(i * piece + b * 32, 32)
            x = hbuf[me, at, :].astype(F32)
            acc[at, :] = x
            inv_rms = lax.rsqrt(jnp.mean(x * x, axis=-1, keepdims=True) + 1e-6)
            hbuf[me, at, :] = (x * inv_rms * gain).astype(BF16)
        if i > 0:
            send_h(i - 1).start()
    for n in range(2, DEPTH):
        start(shared_up(n, n))
    send_h(PIECES - 1).start()
    send_sib().start()

    load_r.wait()
    logits = lax.dot_general(hbuf[me], wr[...], (((1,), (1,)), ((), ())), preferred_element_type=F32)
    prob[me] = jax.nn.softmax(logits, axis=-1)
    wsg = wsg_ref[...].astype(F32)

    @pl.loop(0, tok // 32)
    def _(b):
        at = aligned(b * 32, 32)
        dot = jnp.sum(hbuf[me, at, :].astype(F32) * wsg, axis=-1, keepdims=True)
        sgate[at, :] = jnp.broadcast_to(jax.nn.sigmoid(dot), (32, sgate.shape[1]))

    idx_in[0].wait_recv()
    idx_out[2].start()
    p_out[0].start()
    p_out[1].start()

    def shared_up_step(n):
        s = lax.rem(n, DEPTH)
        wait(shared_up(n, s))
        h = hbuf[me]
        gate = jnp.dot(h, ring[s, 0], preferred_element_type=F32)
        up = jnp.dot(h, ring[s, 1], preferred_element_type=F32)
        act[aligned(n // parts * tok, tok), aligned(lax.rem(n, parts) * WIDTH, WIDTH)] = (jax.nn.silu(gate) * up).astype(BF16)
        issue(n + DEPTH)

    @pl.loop(0, n_s1)
    def _(n):
        shared_up_step(n)

    def pass_on(i):
        take_h(i).wait_recv()
        pass_h(i).start()

    pass_on(0)

    @pl.loop(0, n_s2)
    def _(n):
        s = lax.rem(n_s1 + n, DEPTH)
        wait(shared_down(n, s))
        val = jnp.dot(act[0:tok, :], ring[s, 0, 0:ff, :], preferred_element_type=F32)
        val = val + jnp.dot(act[tok:2 * tok, :], ring[s, 1, 0:ff, :], preferred_element_type=F32)
        cols = aligned(n * WIDTH, WIDTH)
        acc[:, cols] = acc[:, cols] + sgate[:, 0:1] * val
        issue(n_s1 + n + DEPTH)

    pass_on(1)

    for copy in idx_in[1:]:
        copy.wait_recv()
    counts[...] = jnp.zeros_like(counts)
    before = lax.broadcasted_iota(jnp.int32, (tok, tok), 0) < lax.broadcasted_iota(jnp.int32, (tok, tok), 1)
    before = jnp.where(before, 1.0, 0.0).astype(BF16)
    expert_id = lax.broadcasted_iota(jnp.int32, (experts, tok), 0)
    for src in range(group):
        hit = expert_id == idx_all[src, 0:1, :]
        for k in range(1, top_k):
            hit = jnp.logical_or(hit, expert_id == idx_all[src, k:k + 1, :])
        chosen = jnp.where(hit, 1.0, 0.0).astype(F32)
        pos = jnp.dot(chosen.astype(BF16), before, preferred_element_type=F32)
        kept = jnp.logical_and(hit, pos + counts[:, 0:1] < capacity)
        post[src] = jnp.where(kept, pos, -1.0)
        counts[...] = counts[...] + jnp.broadcast_to(jnp.sum(chosen, axis=1, keepdims=True), counts.shape)

    place = lax.broadcasted_iota(jnp.int32, (local_max, tok), 0).astype(F32)

    @pl.loop(0, group)
    def _(src):
        for e in range(slots):
            row = post[src, pl.ds(me * slots + e, 1), :]
            act[aligned(src * width + e * local_max, local_max), 0:tok] = jnp.where(place == row, 1.0, 0.0).astype(BF16)

    def dispatch(src):
        @pl.loop(0, hidden // 256)
        def _(c):
            cols = aligned(c * 256, 256)
            got = jnp.dot(act[aligned(src * width, width), 0:tok], hbuf[src, :, cols], preferred_element_type=F32).astype(BF16)
            for e in range(slots):
                xbuf[aligned(e * rows + src * local_max, local_max), cols] = got[e * local_max:(e + 1) * local_max, :]

    dispatch(me)
    take_sib().wait_recv()
    dispatch(sib)
    for i in range(2, PIECES):
        pass_on(i)
    dispatch(far)
    for i in range(PIECES):
        take_passed(i).wait_recv()
    dispatch(diag)
    p_in[0].wait_recv()
    p_out[2].start()
    p_in[1].wait_recv()
    p_in[2].wait_recv()
    for i in range(PIECES):
        send_h(i).wait_send()
        pass_h(i).wait_send()
    send_sib().wait_send()
    for copy in idx_out + p_out:
        copy.wait_send()

    lane = lax.broadcasted_iota(jnp.int32, (experts, width), 1)
    scale = 65536 // local_max + 1
    slot_of = (lane * scale) // 65536
    spread = jnp.where(lax.broadcasted_iota(jnp.int32, (experts, width), 0) == slot_of + me * slots, 1.0, 0.0).astype(BF16)

    def gates(dst):
        col = lax.broadcasted_iota(jnp.int32, (1, width), 1)
        where = (col - (col * scale) // 65536 * local_max).astype(F32)
        here = lax.dot_general(post[dst].astype(BF16), spread, (((0,), (0,)), ((), ())), preferred_element_type=F32) == where
        rest = prob[dst]
        for i in range(3):
            part = rest.astype(BF16)
            rest = rest - part.astype(F32)
            val = jnp.where(here, jnp.dot(part, spread, preferred_element_type=F32), 0.0).astype(BF16)
            hbuf[dst, :, i * width:(i + 1) * width] = val

    @pl.loop(0, n_g)
    def _(n):
        s = lax.rem(first_g + n, DEPTH)
        wait(expert_up(n, s))
        at = aligned(n // parts * rows, rows)
        x = xbuf[at, :]
        gate = jnp.dot(x, ring[s, 0], preferred_element_type=F32)
        up = jnp.dot(x, ring[s, 1], preferred_element_type=F32)
        act[at, aligned(lax.rem(n, parts) * WIDTH, WIDTH)] = (jax.nn.silu(gate) * up).astype(BF16)
        issue(first_g + n + DEPTH)

        @pl.when(lax.rem(n, n_g // group) == n_g // group - 2)
        def _():
            gates(n // (n_g // group))

    def send_pair(j):
        return remote(pair, fromsib.at[lax.rem(j, 2)], pair_send, pair_recv.at[lax.rem(j, 2)], sib)

    def send_relay(j):
        return remote(relay.at[j], fromchip.at[j], relay_send.at[j], relay_recv.at[j], far)

    def hand_over(j):
        send_pair(j).wait()
        s = lax.rem(j, 2)
        cols = aligned(j * WIDTH, WIDTH)
        relay[j] = relay[j] + fromsib[s, 1]
        send_relay(j).start()
        acc[:, cols] = acc[:, cols] + fromsib[s, 0]

        @pl.when(j < n_chunk - 2)
        def _():
            pl.semaphore_signal(credit, inc=1, device_id={'ep': sib}, device_id_type=MESH)

    def combined(dst):
        mixed = xbuf[aligned(dst * width, width), 0:WIDTH]
        total = jnp.dot(hbuf[dst, :, 0:width], mixed, preferred_element_type=F32)
        for i in range(1, 3):
            total = total + jnp.dot(hbuf[dst, :, i * width:(i + 1) * width], mixed, preferred_element_type=F32)
        return total

    @pl.loop(0, n_d)
    def _(n):
        s = lax.rem(first_d + n, DEPTH)
        j, two = n // n_pair, lax.rem(n, n_pair)
        wait(expert_down(n, s))
        for i in range(2):
            e = two * 2 + i
            res = jnp.dot(act[aligned(e * rows, rows), :], ring[s, i, 0:ff, :], preferred_element_type=F32).astype(BF16)
            for dst in range(group):
                xbuf[aligned(dst * width + e * local_max, local_max), 0:WIDTH] = res[dst * local_max:(dst + 1) * local_max, :]
        issue(first_d + n + DEPTH)

        @pl.when(jnp.logical_and(two == 0, j > 0))
        def _():
            hand_over(j - 1)

        @pl.when(two == n_pair - 1)
        def _():
            pair[0] = combined(sib)
            pair[1] = combined(diag)

            @pl.when(j >= 2)
            def _():
                pl.semaphore_wait(credit, 1)

            send_pair(j).start()
            relay[j] = combined(far)
            cols = aligned(j * WIDTH, WIDTH)
            acc[:, cols] = acc[:, cols] + combined(me)

    hand_over(n_chunk - 1)

    def put(j):
        cols = aligned(j * WIDTH, WIDTH)
        return pltpu.make_async_copy(xbuf.at[0:tok, cols], out_hbm.at[:, cols], out_sem.at[j])

    @pl.loop(0, n_chunk)
    def _(j):
        cols = aligned(j * WIDTH, WIDTH)
        send_relay(j).wait()
        xbuf[0:tok, cols] = (acc[:, cols] + fromchip[j]).astype(BF16)
        put(j).start()

    @pl.loop(0, n_chunk)
    def _(j):
        put(j).wait()


def moe(hidden_in, idx_t, gain, w_router, wsg, s_gate, s_up, s_down, w_gate, w_up, w_down, group, capacity, local_max):
    tok, hidden = hidden_in.shape
    slots, _, ff = w_gate.shape
    experts = w_router.shape[0]
    rows = group * local_max
    chunks = hidden // WIDTH
    vmem, dma = pltpu.VMEM, pltpu.SemaphoreType.DMA
    hbm_spec, vmem_spec = pl.BlockSpec(memory_space=pl.ANY), pl.BlockSpec(memory_space=pltpu.VMEM)
    return pl.pallas_call(
        functools.partial(moe_kernel, group, experts, capacity, local_max),
        out_shape=jax.ShapeDtypeStruct((tok, hidden), BF16),
        in_specs=[hbm_spec, vmem_spec, vmem_spec, hbm_spec, vmem_spec] + [hbm_spec] * 6,
        out_specs=hbm_spec,
        scratch_shapes=[
            vmem((DEPTH, 2, hidden, WIDTH), BF16),
            vmem((slots * rows, hidden), BF16),
            vmem((slots * rows, ff), BF16),
            vmem((group, tok, hidden), BF16),
            vmem((2, tok, WIDTH), F32),
            vmem((chunks, tok, WIDTH), F32),
            vmem((2, 2, tok, WIDTH), F32),
            vmem((chunks, tok, WIDTH), F32),
            vmem((tok, hidden), F32),
            vmem((group, tok, experts), F32),
            vmem((group, experts, tok), F32),
            vmem((tok, 128), F32),
            vmem((group,) + idx_t.shape, jnp.int32),
            vmem((experts, hidden), BF16),
            vmem((experts, 128), F32),
            dma((DEPTH, 2)), dma((2,)), dma((chunks,)),
            dma((3,)), dma((3,)), dma((PIECES,)), dma((PIECES,)), dma, dma, dma((PIECES,)), dma((PIECES,)),
            dma((3,)), dma((3,)), dma, dma((2,)), dma((chunks,)), dma((chunks,)), pltpu.SemaphoreType.REGULAR,
        ],
        compiler_params=pltpu.CompilerParams(collective_id=0, has_side_effects=True, vmem_limit_bytes=67043328),
        cost_estimate=pl.CostEstimate(flops=6 * slots * rows * hidden * ff, bytes_accessed=6 * slots * hidden * ff, transcendentals=0),
        name="moe",
    )(hidden_in, idx_t, gain, w_router, wsg, s_gate, s_up, s_down, w_gate, w_up, w_down)


def solution(mesh):
    group = mesh.shape['ep']

    def device_block(hidden_in, topk_idx, norm_gain, w_router, w_sgate, s_gate, s_up, s_down, w_gate, w_up, w_down):
        tok_dev, hidden = hidden_in.shape
        top_k = topk_idx.shape[1]
        experts = w_router.shape[1]
        capacity = (5 * tok_dev * group * top_k + 4 * experts - 1) // (4 * experts)
        local_max = (2 * tok_dev * top_k + experts - 1) // experts
        return moe(hidden_in, topk_idx.T, norm_gain, w_router.T, w_sgate.reshape(1, hidden),
                   s_gate, s_up, s_down, w_gate, w_up, w_down, group, capacity, local_max)

    row_spec = P(('dp', 'ep'), None)
    full_spec = P(None, None)
    slot_spec = P('ep', None, None)
    in_specs = (row_spec, row_spec, P(None), full_spec, full_spec, full_spec, full_spec, full_spec,
                slot_spec, slot_spec, slot_spec)
    return jax.shard_map(device_block, mesh=mesh, in_specs=in_specs, out_specs=row_spec, check_vma=False)
```

time: 754 us -> 185 us (0.25)
  matrix products: 192 us -> 0 us
  Pallas kernels: 0 us -> 183 us
  blocking collectives: 182 us -> 0 us
  waiting for transfers between devices: 139 us -> 0 us
  local copies, waits for them, and re-layouts: 126 us -> 2.46 us
  other arithmetic: 101 us -> 0 us
    dot_general x8 -> x0, matrix products: 192 us -> none  [the longest x1 56.1 us: device_block(): jnp.einsum('sch,shf->scf', recv_buf, w_up, preferred_element_type=jnp.flo...]
    pallas_call x0 -> x1, Pallas kernels: none -> 183 us  [moe(): pl.pallas_call(functools.partial(moe_kernel, group, experts, capacity, lo...]
    all_to_all x1 -> x0, blocking collectives: 175 us -> none  [device_block(): recv_buf = lax.all_to_all(send_buf, 'ep', 0, 1, tiled=True)]
    all_to_all x1 -> x0, waiting for transfers between devices: 139 us -> none  [device_block(): back_buf = lax.all_to_all(expert_out, 'ep', 1, 0, tiled=True)]
    gather x14 -> x0, local copies, waits for them, and re-layouts: 69 us -> none  [the longest x2 35.9 us: device_block(): jnp.take(back_buf.reshape(num_slots * local_max, hidden), buf_pos, axis=0...]
    gather x6 -> x0, other arithmetic: 41.1 us -> none  [the longest x3 41.1 us: device_block(): global_pos = jnp.take(lower_counts, flat_ids) + local_pos]
    reduce_sum x5 -> x0, other arithmetic: 30.8 us -> none  [the longest x1 28.8 us: device_block(): routed = jnp.sum(gate_vals[:, :, None] * picked.astype(jnp.float32), axis=1)]
    convert_element_type x1 -> x0, local copies, waits for them, and re-layouts: 23.4 us -> none  [device_block(): jnp.einsum('scf,sfh->sch', expert_act, w_down, preferred_element_type=jnp...]
  transfers between devices with their start and end apart: 1 -> 0, of which waited for: 1 -> 0; matrix products, arithmetic and copies ran while one was open for 4% -> 0% of each run, Pallas kernels for 0% -> 0%
where the time goes in v2:
time: 185 us
  Pallas kernels  183 us (99%)
  local copies, waits for them, and re-layouts  2.46 us (1%)
    pallas_call x1, Pallas kernels, moe(): pl.pallas_call(functools.partial(moe_kernel, group, experts, capacity, lo...  183 us

profile of v2, /device:TPU:0, one launch (start us, length us, event | category | flops | bytes accessed | tf_op | source)
XLA Modules:
  0.0 185.2 jit_solution(12925338403873802972)
XLA Ops:
  0.0 182.7 %moe.1 = bf16[256,2560]{1,0:T(8,128)(2,1)} custom-call(bf16[256,2560]{1,0:T(8,128)(2,1)} %x_hbm.1, s32[6,256]{1,0:T(8,128)} %bitcast.5, bf16[2560]{0:T(1024)(128)(2,1)} %gain_ref.1, bf16[64,2560]{1,0:T(8,128)(2,1)} %bitcast.3, bf16[1,2560]{1,0:T(2,128)(2,1)} %bitcast.4, bf16[2560,3072]{1,0:T(8,128)(2,1)} %sg_hbm.1, bf16[2560,3072]{1,0:T(8,128)(2,1)} %su_hbm.1, ...), custom_call_target="tpu_custom_call" | custom-call | flops 72477573120 | bytes 377487360 | tf_op jit(solution)/shard_map/moe/pallas_call | solution.py:375
  182.8 2.5 %copy.13 = bf16[256,2560]{1,0:T(8,128)(2,1)} copy(bf16[256,2560]{1,0:T(8,128)(2,1)} %moe.1) | data formatting | bytes 2621440

commit v3 on v2

--- a/solution.py
+++ b/solution.py
@@ -12,7 +12,10 @@
 MESH = pl.DeviceIdType.MESH
 DEPTH = 4
 WIDTH = 512
-PIECES = 4
+PIECES = 5
+EARLY = 3
+AHEAD = 8
+CHUNK = 256
 
 
 def aligned(start, size):
@@ -22,9 +25,9 @@
 def moe_kernel(group, experts, capacity, local_max,
                x_hbm, idx_ref, gain_ref, wr_hbm, wsg_ref, sg_hbm, su_hbm, sd_hbm, wg_hbm, wu_hbm, wd_hbm,
                out_hbm,
-               ring, xbuf, act, hbuf, pair, relay, fromsib, fromchip, acc, prob, post, sgate, idx_all, wr, counts,
+               ring, xbuf, act, hbuf, work, acc, prob, post, sgate, idx_all, wr, counts,
                ring_sem, in_sem, out_sem, idx_send, idx_recv, h_send, h_recv, sib_send, sib_recv, fwd_send, fwd_recv,
-               p_send, p_recv, pair_send, pair_recv, relay_send, relay_recv, credit):
+               p_send, p_recv, pair_send, pair_recv, relay_send, relay_recv, credit, ready):
     tok, hidden = x_hbm.shape
     slots, _, ff = wg_hbm.shape
     top_k = idx_ref.shape[0]
@@ -33,13 +36,16 @@
     n_s1 = 2 * ff // WIDTH
     n_s2 = hidden // WIDTH
     parts = ff // WIDTH
-    n_g = slots * parts
-    n_chunk = hidden // WIDTH
-    n_pair = slots // 2
-    n_d = n_chunk * n_pair
-    first_g, first_d = n_s1 + n_s2, n_s1 + n_s2 + n_g
+    n_full = slots * parts - AHEAD
+    n_chunk = hidden // CHUNK
+    quads = slots // 4
+    n_d = n_chunk * quads
+    first_a = n_s1 + n_s2
+    first_b, first_g = first_a + AHEAD, first_a + 2 * AHEAD
+    first_d = first_g + n_full
     total = first_d + n_d
-    piece = tok // PIECES
+    piece = hidden // PIECES
+    k_early = EARLY * piece
 
     me = lax.axis_index('ep')
     sib = me + 1 - 2 * lax.rem(me, 2)
@@ -56,15 +62,17 @@
         return tuple(pltpu.make_async_copy(sd_hbm.at[i * ff:(i + 1) * ff, cols], ring.at[s, i, 0:ff, :], ring_sem.at[s, i])
                      for i in range(2))
 
-    def expert_up(n, s):
+    def expert_up(n, s, low=0, high=hidden):
         e, cols = n // parts, aligned(lax.rem(n, parts) * WIDTH, WIDTH)
-        return (pltpu.make_async_copy(wg_hbm.at[e, :, cols], ring.at[s, 0], ring_sem.at[s, 0]),
-                pltpu.make_async_copy(wu_hbm.at[e, :, cols], ring.at[s, 1], ring_sem.at[s, 1]))
+        return tuple(pltpu.make_async_copy(w.at[e, low:high, cols], ring.at[s, i, 0:high - low, :], ring_sem.at[s, i])
+                     for i, w in enumerate((wg_hbm, wu_hbm)))
 
     def expert_down(n, s):
-        e, cols = lax.rem(n, n_pair) * 2, aligned(n // n_pair * WIDTH, WIDTH)
-        return tuple(pltpu.make_async_copy(wd_hbm.at[e + i, :, cols], ring.at[s, i, 0:ff, :], ring_sem.at[s, i])
-                     for i in range(2))
+        e, cols = lax.rem(n, quads) * 4, aligned(n // quads * CHUNK, CHUNK)
+        return tuple(pltpu.make_async_copy(wd_hbm.at[e + i, :, cols], down_part(s, i), ring_sem.at[s, i]) for i in range(4))
+
+    def down_part(s, i):
+        return ring.at[s, i // 2, 0:ff, i % 2 * CHUNK:(i % 2 + 1) * CHUNK]
 
     def start(copies):
         for copy in copies:
@@ -81,13 +89,21 @@
         def _():
             start(shared_up(n, s))
 
-        @pl.when(jnp.logical_and(n >= n_s1, n < first_g))
+        @pl.when(jnp.logical_and(n >= n_s1, n < first_a))
         def _():
             start(shared_down(n - n_s1, s))
 
+        @pl.when(jnp.logical_and(n >= first_a, n < first_b))
+        def _():
+            start(expert_up(n - first_a, s, 0, k_early))
+
+        @pl.when(jnp.logical_and(n >= first_b, n < first_g))
+        def _():
+            start(expert_up(n - first_b, s, k_early, hidden))
+
         @pl.when(jnp.logical_and(n >= first_g, n < first_d))
         def _():
-            start(expert_up(n - first_g, s))
+            start(expert_up(n - first_g + AHEAD, s))
 
         @pl.when(jnp.logical_and(n >= first_d, n < total))
         def _():
@@ -98,7 +114,7 @@
                                             device_id={'ep': to}, device_id_type=MESH)
 
     def h_piece(owner, i):
-        return hbuf.at[owner, i * piece:(i + 1) * piece, :]
+        return hbuf.at[owner, :, i * piece:(i + 1) * piece]
 
     def send_h(i):
         return remote(h_piece(me, i), h_piece(me, i), h_send.at[i], h_recv.at[i], far)
@@ -145,15 +161,22 @@
     idx_out[0].start()
     idx_out[1].start()
 
+    @pl.loop(0, tok // 32)
+    def _(b):
+        at = aligned(b * 32, 32)
+        x = hbuf[me, at, :].astype(F32)
+        acc[at, :] = x
+        inv_rms = lax.rsqrt(jnp.mean(x * x, axis=-1, keepdims=True) + 1e-6)
+        sgate[at, :] = jnp.broadcast_to(inv_rms, (32, sgate.shape[1]))
+
     gain = gain_ref[...].astype(F32).reshape(1, hidden)
     for i in range(PIECES):
-        @pl.loop(0, piece // 32)
+        cols = slice(i * piece, (i + 1) * piece)
+
+        @pl.loop(0, tok // 64)
         def _(b):
-            at = aligned(i * piece + b * 32, 32)
-            x = hbuf[me, at, :].astype(F32)
-            acc[at, :] = x
-            inv_rms = lax.rsqrt(jnp.mean(x * x, axis=-1, keepdims=True) + 1e-6)
-            hbuf[me, at, :] = (x * inv_rms * gain).astype(BF16)
+            at = aligned(b * 64, 64)
+            hbuf[me, at, cols] = (acc[at, cols] * sgate[at, 0:1] * gain[:, cols]).astype(BF16)
         if i > 0:
             send_h(i - 1).start()
     for n in range(2, DEPTH):
@@ -161,9 +184,6 @@
     send_h(PIECES - 1).start()
     send_sib().start()
 
-    load_r.wait()
-    logits = lax.dot_general(hbuf[me], wr[...], (((1,), (1,)), ((), ())), preferred_element_type=F32)
-    prob[me] = jax.nn.softmax(logits, axis=-1)
     wsg = wsg_ref[...].astype(F32)
 
     @pl.loop(0, tok // 32)
@@ -174,8 +194,6 @@
 
     idx_in[0].wait_recv()
     idx_out[2].start()
-    p_out[0].start()
-    p_out[1].start()
 
     def shared_up_step(n):
         s = lax.rem(n, DEPTH)
@@ -232,32 +250,78 @@
             row = post[src, pl.ds(me * slots + e, 1), :]
             act[aligned(src * width + e * local_max, local_max), 0:tok] = jnp.where(place == row, 1.0, 0.0).astype(BF16)
 
-    def dispatch(src):
-        @pl.loop(0, hidden // 256)
+    def dispatch(src, low, high, step=1):
+        @pl.loop(low // step, high // step)
         def _(c):
-            cols = aligned(c * 256, 256)
-            got = jnp.dot(act[aligned(src * width, width), 0:tok], hbuf[src, :, cols], preferred_element_type=F32).astype(BF16)
-            for e in range(slots):
-                xbuf[aligned(e * rows + src * local_max, local_max), cols] = got[e * local_max:(e + 1) * local_max, :]
-
-    dispatch(me)
+            cols = aligned(c * step * piece, step * piece)
+            for first in range(0, slots, 4):
+                pick = act[aligned(src * width + first * local_max, 4 * local_max), 0:tok]
+                got = jnp.dot(pick, hbuf[src, :, cols], preferred_element_type=F32).astype(BF16)
+                for e in range(4):
+                    xbuf[aligned((first + e) * rows + src * local_max, local_max), cols] = got[e * local_max:(e + 1) * local_max, :]
+
+    def rows_of(u):
+        return aligned(u // parts * rows, rows)
+
+    def expert_a(u):
+        s = lax.rem(first_a + u, DEPTH)
+        wait(expert_up(u, s, 0, k_early))
+        x = xbuf[rows_of(u), 0:k_early]
+        for i in range(2):
+            res = jnp.dot(x, ring[s, i, 0:k_early, :], preferred_element_type=F32)
+            for half in range(2):
+                work[4 * u + 2 * i + half, 0:rows, :] = res[:, half * CHUNK:(half + 1) * CHUNK]
+        issue(first_a + u + DEPTH)
+
+    dispatch(me, 0, PIECES)
     take_sib().wait_recv()
-    dispatch(sib)
-    for i in range(2, PIECES):
+    dispatch(sib, 0, PIECES)
+    for i in range(2, EARLY):
         pass_on(i)
-    dispatch(far)
-    for i in range(PIECES):
+    dispatch(far, 0, EARLY)
+    for i in range(EARLY):
         take_passed(i).wait_recv()
-    dispatch(diag)
-    p_in[0].wait_recv()
-    p_out[2].start()
-    p_in[1].wait_recv()
-    p_in[2].wait_recv()
+    dispatch(diag, 0, EARLY)
+
+    @pl.loop(0, AHEAD // 2)
+    def _(u):
+        expert_a(u)
+
+    pass_on(EARLY)
+    dispatch(far, EARLY, EARLY + 1)
+
+    @pl.loop(AHEAD // 2, AHEAD)
+    def _(u):
+        expert_a(u)
+
+    take_passed(EARLY).wait_recv()
+    dispatch(diag, EARLY, EARLY + 1)
+    pass_on(EARLY + 1)
+    dispatch(far, EARLY + 1, PIECES)
+    take_passed(EARLY + 1).wait_recv()
+    dispatch(diag, EARLY + 1, PIECES)
+
+    @pl.loop(0, AHEAD)
+    def _(u):
+        s = lax.rem(first_b + u, DEPTH)
+        wait(expert_up(u, s, k_early, hidden))
+        x = xbuf[rows_of(u), k_early:hidden]
+        gate = jnp.dot(x, ring[s, 0, 0:hidden - k_early, :], preferred_element_type=F32)
+        up = jnp.dot(x, ring[s, 1, 0:hidden - k_early, :], preferred_element_type=F32)
+        for half in range(2):
+            cols = slice(half * CHUNK, (half + 1) * CHUNK)
+            g = work[4 * u + half, 0:rows, :] + gate[:, cols]
+            v = work[4 * u + 2 + half, 0:rows, :] + up[:, cols]
+            act[rows_of(u), aligned(lax.rem(u, parts) * WIDTH + half * CHUNK, CHUNK)] = (jax.nn.silu(g) * v).astype(BF16)
+        issue(first_b + u + DEPTH)
+
+    pl.semaphore_signal(credit, inc=2, device_id={'ep': sib}, device_id_type=MESH)
+    pl.semaphore_signal(ready, inc=1, device_id={'ep': far}, device_id_type=MESH)
     for i in range(PIECES):
         send_h(i).wait_send()
         pass_h(i).wait_send()
     send_sib().wait_send()
-    for copy in idx_out + p_out:
+    for copy in idx_out:
         copy.wait_send()
 
     lane = lax.broadcasted_iota(jnp.int32, (experts, width), 1)
@@ -276,41 +340,70 @@
             val = jnp.where(here, jnp.dot(part, spread, preferred_element_type=F32), 0.0).astype(BF16)
             hbuf[dst, :, i * width:(i + 1) * width] = val
 
-    @pl.loop(0, n_g)
+    @pl.loop(0, n_full)
     def _(n):
         s = lax.rem(first_g + n, DEPTH)
-        wait(expert_up(n, s))
-        at = aligned(n // parts * rows, rows)
-        x = xbuf[at, :]
+        u = n + AHEAD
+        wait(expert_up(u, s))
+        x = xbuf[rows_of(u), :]
         gate = jnp.dot(x, ring[s, 0], preferred_element_type=F32)
         up = jnp.dot(x, ring[s, 1], preferred_element_type=F32)
-        act[at, aligned(lax.rem(n, parts) * WIDTH, WIDTH)] = (jax.nn.silu(gate) * up).astype(BF16)
+        act[rows_of(u), aligned(lax.rem(u, parts) * WIDTH, WIDTH)] = (jax.nn.silu(gate) * up).astype(BF16)
         issue(first_g + n + DEPTH)
 
-        @pl.when(lax.rem(n, n_g // group) == n_g // group - 2)
-        def _():
-            gates(n // (n_g // group))
+        @pl.when(n == 0)
+        def _():
+            load_r.wait()
+            logits = lax.dot_general(hbuf[me], wr[...], (((1,), (1,)), ((), ())), preferred_element_type=F32)
+            prob[me] = jax.nn.softmax(logits, axis=-1)
+
+        @pl.when(n == 1)
+        def _():
+            p_out[0].start()
+            p_out[1].start()
+
+        @pl.when(n == 4)
+        def _():
+            p_in[0].wait_recv()
+            p_out[2].start()
+
+        @pl.when(n == 6)
+        def _():
+            for copy in p_in[1:]:
+                copy.wait_recv()
+            for copy in p_out:
+                copy.wait_send()
+
+        @pl.when(lax.rem(n, n_full // group) == n_full // group - 2)
+        def _():
+            gates(n // (n_full // group))
 
     def send_pair(j):
-        return remote(pair, fromsib.at[lax.rem(j, 2)], pair_send, pair_recv.at[lax.rem(j, 2)], sib)
+        at = 2 * n_chunk
+        return remote(work.at[at + 4:at + 6], work.at[pl.ds(at + 2 * lax.rem(j, 2), 2)], pair_send, pair_recv.at[lax.rem(j, 2)], sib)
 
     def send_relay(j):
-        return remote(relay.at[j], fromchip.at[j], relay_send.at[j], relay_recv.at[j], far)
+        return remote(work.at[j], work.at[n_chunk + j], relay_send.at[j], relay_recv.at[j], far)
 
     def hand_over(j):
         send_pair(j).wait()
-        s = lax.rem(j, 2)
-        cols = aligned(j * WIDTH, WIDTH)
-        relay[j] = relay[j] + fromsib[s, 1]
+        got = 2 * n_chunk + 2 * lax.rem(j, 2)
+        cols = aligned(j * CHUNK, CHUNK)
+        work[j] = work[j] + work[got + 1]
+        acc[:, cols] = acc[:, cols] + work[got]
+
+        @pl.when(j == 0)
+        def _():
+            pl.semaphore_wait(ready, 1)
+
         send_relay(j).start()
-        acc[:, cols] = acc[:, cols] + fromsib[s, 0]
 
         @pl.when(j < n_chunk - 2)
         def _():
             pl.semaphore_signal(credit, inc=1, device_id={'ep': sib}, device_id_type=MESH)
 
     def combined(dst):
-        mixed = xbuf[aligned(dst * width, width), 0:WIDTH]
+        mixed = xbuf[aligned(dst * width, width), 0:CHUNK]
         total = jnp.dot(hbuf[dst, :, 0:width], mixed, preferred_element_type=F32)
         for i in range(1, 3):
             total = total + jnp.dot(hbuf[dst, :, i * width:(i + 1) * width], mixed, preferred_element_type=F32)
@@ -319,44 +412,44 @@
     @pl.loop(0, n_d)
     def _(n):
         s = lax.rem(first_d + n, DEPTH)
-        j, two = n // n_pair, lax.rem(n, n_pair)
+        j, quad = n // quads, lax.rem(n, quads)
         wait(expert_down(n, s))
-        for i in range(2):
-            e = two * 2 + i
-            res = jnp.dot(act[aligned(e * rows, rows), :], ring[s, i, 0:ff, :], preferred_element_type=F32).astype(BF16)
+        for i in range(4):
+            e = quad * 4 + i
+            res = jnp.dot(act[aligned(e * rows, rows), :], down_part(s, i)[...], preferred_element_type=F32).astype(BF16)
             for dst in range(group):
-                xbuf[aligned(dst * width + e * local_max, local_max), 0:WIDTH] = res[dst * local_max:(dst + 1) * local_max, :]
+                xbuf[aligned(dst * width + e * local_max, local_max), 0:CHUNK] = res[dst * local_max:(dst + 1) * local_max, :]
         issue(first_d + n + DEPTH)
 
-        @pl.when(jnp.logical_and(two == 0, j > 0))
+        @pl.when(jnp.logical_and(quad == 0, j > 1))
         def _():
             hand_over(j - 1)
 
-        @pl.when(two == n_pair - 1)
-        def _():
-            pair[0] = combined(sib)
-            pair[1] = combined(diag)
-
-            @pl.when(j >= 2)
+        @pl.when(quad == quads - 1)
+        def _():
+            work[2 * n_chunk + 4] = combined(sib)
+            work[2 * n_chunk + 5] = combined(diag)
+            pl.semaphore_wait(credit, 1)
+            send_pair(j).start()
+            work[j] = combined(far)
+            cols = aligned(j * CHUNK, CHUNK)
+            acc[:, cols] = acc[:, cols] + combined(me)
+
+            @pl.when(j == 0)
             def _():
-                pl.semaphore_wait(credit, 1)
-
-            send_pair(j).start()
-            relay[j] = combined(far)
-            cols = aligned(j * WIDTH, WIDTH)
-            acc[:, cols] = acc[:, cols] + combined(me)
+                hand_over(0)
 
     hand_over(n_chunk - 1)
 
     def put(j):
-        cols = aligned(j * WIDTH, WIDTH)
+        cols = aligned(j * CHUNK, CHUNK)
         return pltpu.make_async_copy(xbuf.at[0:tok, cols], out_hbm.at[:, cols], out_sem.at[j])
 
     @pl.loop(0, n_chunk)
     def _(j):
-        cols = aligned(j * WIDTH, WIDTH)
+        cols = aligned(j * CHUNK, CHUNK)
         send_relay(j).wait()
-        xbuf[0:tok, cols] = (acc[:, cols] + fromchip[j]).astype(BF16)
+        xbuf[0:tok, cols] = (acc[:, cols] + work[n_chunk + j]).astype(BF16)
         put(j).start()
 
     @pl.loop(0, n_chunk)
@@ -369,7 +462,7 @@
     slots, _, ff = w_gate.shape
     experts = w_router.shape[0]
     rows = group * local_max
-    chunks = hidden // WIDTH
+    chunks = hidden // CHUNK
     vmem, dma = pltpu.VMEM, pltpu.SemaphoreType.DMA
     hbm_spec, vmem_spec = pl.BlockSpec(memory_space=pl.ANY), pl.BlockSpec(memory_space=pltpu.VMEM)
     return pl.pallas_call(
@@ -382,10 +475,7 @@
             vmem((slots * rows, hidden), BF16),
             vmem((slots * rows, ff), BF16),
             vmem((group, tok, hidden), BF16),
-            vmem((2, tok, WIDTH), F32),
-            vmem((chunks, tok, WIDTH), F32),
-            vmem((2, 2, tok, WIDTH), F32),
-            vmem((chunks, tok, WIDTH), F32),
+            vmem((max(2 * chunks + 6, 4 * AHEAD), tok, CHUNK), F32),
             vmem((tok, hidden), F32),
             vmem((group, tok, experts), F32),
             vmem((group, experts, tok), F32),
@@ -393,9 +483,9 @@
             vmem((group,) + idx_t.shape, jnp.int32),
             vmem((experts, hidden), BF16),
             vmem((experts, 128), F32),
-            dma((DEPTH, 2)), dma((2,)), dma((chunks,)),
+            dma((DEPTH, 4)), dma((2,)), dma((chunks,)),
             dma((3,)), dma((3,)), dma((PIECES,)), dma((PIECES,)), dma, dma, dma((PIECES,)), dma((PIECES,)),
-            dma((3,)), dma((3,)), dma, dma((2,)), dma((chunks,)), dma((chunks,)), pltpu.SemaphoreType.REGULAR,
+            dma((3,)), dma((3,)), dma, dma((2,)), dma((chunks,)), dma((chunks,)), pltpu.SemaphoreType.REGULAR, pltpu.SemaphoreType.REGULAR,
         ],
         compiler_params=pltpu.CompilerParams(collective_id=0, has_side_effects=True, vmem_limit_bytes=67043328),
         cost_estimate=pl.CostEstimate(flops=6 * slots * rows * hidden * ff, bytes_accessed=6 * slots * hidden * ff, transcendentals=0),

time: 185 us -> 173 us (0.935)
  Pallas kernels: 183 us -> 170 us
    pallas_call x1, Pallas kernels: 183 us -> 170 us  [moe(): pl.pallas_call(functools.partial(moe_kernel, group, experts, capacity, lo...]
where the time goes in v3:
time: 173 us; the launch traced here: 172 us
  Pallas kernels  170 us (98%)
  local copies, waits for them, and re-layouts  2.46 us (1%)
    pallas_call x1, Pallas kernels, moe(): pl.pallas_call(functools.partial(moe_kernel, group, experts, capacity, lo...  170 us

profile of v3, /device:TPU:0, one launch (start us, length us, event | category | flops | bytes accessed | tf_op | source)
XLA Modules:
  0.0 172.3 jit_solution(8840529608960162959)
XLA Ops:
  0.0 169.8 %moe.1 = bf16[256,2560]{1,0:T(8,128)(2,1)} custom-call(bf16[256,2560]{1,0:T(8,128)(2,1)} %x_hbm.1, s32[6,256]{1,0:T(8,128)} %bitcast.5, bf16[2560]{0:T(1024)(128)(2,1)} %gain_ref.1, bf16[64,2560]{1,0:T(8,128)(2,1)} %bitcast.3, bf16[1,2560]{1,0:T(2,128)(2,1)} %bitcast.4, bf16[2560,3072]{1,0:T(8,128)(2,1)} %sg_hbm.1, bf16[2560,3072]{1,0:T(8,128)(2,1)} %su_hbm.1, ...), custom_call_target="tpu_custom_call" | custom-call | flops 72477573120 | bytes 377487360 | tf_op jit(solution)/shard_map/moe/pallas_call | solution.py:468
  169.9 2.5 %copy.13 = bf16[256,2560]{1,0:T(8,128)(2,1)} copy(bf16[256,2560]{1,0:T(8,128)(2,1)} %moe.1) | data formatting | bytes 2621440

commit v4 on v3

--- a/solution.py
+++ b/solution.py
@@ -15,6 +15,7 @@
 PIECES = 5
 EARLY = 3
 AHEAD = 8
+BETWEEN = 4
 CHUNK = 256
 
 
@@ -41,8 +42,10 @@
     quads = slots // 4
     n_d = n_chunk * quads
     first_a = n_s1 + n_s2
-    first_b, first_g = first_a + AHEAD, first_a + 2 * AHEAD
-    first_d = first_g + n_full
+    first_m = first_a + AHEAD
+    first_b = first_m + BETWEEN
+    first_g = first_b + AHEAD
+    first_d = first_g + n_full - BETWEEN
     total = first_d + n_d
     piece = hidden // PIECES
     k_early = EARLY * piece
@@ -93,17 +96,21 @@
         def _():
             start(shared_down(n - n_s1, s))
 
-        @pl.when(jnp.logical_and(n >= first_a, n < first_b))
+        @pl.when(jnp.logical_and(n >= first_a, n < first_m))
         def _():
             start(expert_up(n - first_a, s, 0, k_early))
 
+        @pl.when(jnp.logical_and(n >= first_m, n < first_b))
+        def _():
+            start(expert_up(n - first_m + AHEAD, s))
+
         @pl.when(jnp.logical_and(n >= first_b, n < first_g))
         def _():
             start(expert_up(n - first_b, s, k_early, hidden))
 
         @pl.when(jnp.logical_and(n >= first_g, n < first_d))
         def _():
-            start(expert_up(n - first_g + AHEAD, s))
+            start(expert_up(n - first_g + BETWEEN + AHEAD, s))
 
         @pl.when(jnp.logical_and(n >= first_d, n < total))
         def _():
@@ -161,13 +168,13 @@
     idx_out[0].start()
     idx_out[1].start()
 
-    @pl.loop(0, tok // 32)
+    @pl.loop(0, tok // 64)
     def _(b):
-        at = aligned(b * 32, 32)
+        at = aligned(b * 64, 64)
         x = hbuf[me, at, :].astype(F32)
         acc[at, :] = x
         inv_rms = lax.rsqrt(jnp.mean(x * x, axis=-1, keepdims=True) + 1e-6)
-        sgate[at, :] = jnp.broadcast_to(inv_rms, (32, sgate.shape[1]))
+        sgate[at, :] = jnp.broadcast_to(inv_rms, (64, sgate.shape[1]))
 
     gain = gain_ref[...].astype(F32).reshape(1, hidden)
     for i in range(PIECES):
@@ -301,6 +308,63 @@
     take_passed(EARLY + 1).wait_recv()
     dispatch(diag, EARLY + 1, PIECES)
 
+    lane = lax.broadcasted_iota(jnp.int32, (experts, width), 1)
+    scale = 65536 // local_max + 1
+    slot_of = (lane * scale) // 65536
+    spread = jnp.where(lax.broadcasted_iota(jnp.int32, (experts, width), 0) == slot_of + me * slots, 1.0, 0.0).astype(BF16)
+
+    def gates(dst):
+        col = lax.broadcasted_iota(jnp.int32, (1, width), 1)
+        where = (col - (col * scale) // 65536 * local_max).astype(F32)
+        here = lax.dot_general(post[dst].astype(BF16), spread, (((0,), (0,)), ((), ())), preferred_element_type=F32) == where
+        rest = prob[dst]
+        for i in range(3):
+            part = rest.astype(BF16)
+            rest = rest - part.astype(F32)
+            val = jnp.where(here, jnp.dot(part, spread, preferred_element_type=F32), 0.0).astype(BF16)
+            hbuf[dst, :, i * width:(i + 1) * width] = val
+
+    def expert_whole(n, first):
+        s = lax.rem(first + n, DEPTH)
+        u = n + AHEAD
+        wait(expert_up(u, s))
+        x = xbuf[rows_of(u), :]
+        gate = jnp.dot(x, ring[s, 0], preferred_element_type=F32)
+        up = jnp.dot(x, ring[s, 1], preferred_element_type=F32)
+        act[rows_of(u), aligned(lax.rem(u, parts) * WIDTH, WIDTH)] = (jax.nn.silu(gate) * up).astype(BF16)
+        issue(first + n + DEPTH)
+
+        @pl.when(n == 0)
+        def _():
+            load_r.wait()
+            logits = lax.dot_general(hbuf[me], wr[...], (((1,), (1,)), ((), ())), preferred_element_type=F32)
+            prob[me] = jax.nn.softmax(logits, axis=-1)
+
+        @pl.when(n == 1)
+        def _():
+            p_out[0].start()
+            p_out[1].start()
+
+        @pl.when(n == 4)
+        def _():
+            p_in[0].wait_recv()
+            p_out[2].start()
+
+        @pl.when(n == 6)
+        def _():
+            for copy in p_in[1:]:
+                copy.wait_recv()
+            for copy in p_out:
+                copy.wait_send()
+
+        @pl.when(lax.rem(n, n_full // group) == n_full // group - 2)
+        def _():
+            gates(n // (n_full // group))
+
+    @pl.loop(0, BETWEEN)
+    def _(n):
+        expert_whole(n, first_m)
+
     @pl.loop(0, AHEAD)
     def _(u):
         s = lax.rem(first_b + u, DEPTH)
@@ -324,59 +388,9 @@
     for copy in idx_out:
         copy.wait_send()
 
-    lane = lax.broadcasted_iota(jnp.int32, (experts, width), 1)
-    scale = 65536 // local_max + 1
-    slot_of = (lane * scale) // 65536
-    spread = jnp.where(lax.broadcasted_iota(jnp.int32, (experts, width), 0) == slot_of + me * slots, 1.0, 0.0).astype(BF16)
-
-    def gates(dst):
-        col = lax.broadcasted_iota(jnp.int32, (1, width), 1)
-        where = (col - (col * scale) // 65536 * local_max).astype(F32)
-        here = lax.dot_general(post[dst].astype(BF16), spread, (((0,), (0,)), ((), ())), preferred_element_type=F32) == where
-        rest = prob[dst]
-        for i in range(3):
-            part = rest.astype(BF16)
-            rest = rest - part.astype(F32)
-            val = jnp.where(here, jnp.dot(part, spread, preferred_element_type=F32), 0.0).astype(BF16)
-            hbuf[dst, :, i * width:(i + 1) * width] = val
-
-    @pl.loop(0, n_full)
+    @pl.loop(BETWEEN, n_full)
     def _(n):
-        s = lax.rem(first_g + n, DEPTH)
-        u = n + AHEAD
-        wait(expert_up(u, s))
-        x = xbuf[rows_of(u), :]
-        gate = jnp.dot(x, ring[s, 0], preferred_element_type=F32)
-        up = jnp.dot(x, ring[s, 1], preferred_element_type=F32)
-        act[rows_of(u), aligned(lax.rem(u, parts) * WIDTH, WIDTH)] = (jax.nn.silu(gate) * up).astype(BF16)
-        issue(first_g + n + DEPTH)
-
-        @pl.when(n == 0)
-        def _():
-            load_r.wait()
-            logits = lax.dot_general(hbuf[me], wr[...], (((1,), (1,)), ((), ())), preferred_element_type=F32)
-            prob[me] = jax.nn.softmax(logits, axis=-1)
-
-        @pl.when(n == 1)
-        def _():
-            p_out[0].start()
-            p_out[1].start()
-
-        @pl.when(n == 4)
-        def _():
-            p_in[0].wait_recv()
-            p_out[2].start()
-
-        @pl.when(n == 6)
-        def _():
-            for copy in p_in[1:]:
-                copy.wait_recv()
-            for copy in p_out:
-                copy.wait_send()
-
-        @pl.when(lax.rem(n, n_full // group) == n_full // group - 2)
-        def _():
-            gates(n // (n_full // group))
+        expert_whole(n, first_g - BETWEEN)
 
     def send_pair(j):
         at = 2 * n_chunk

time: 173 us -> 172 us (level)
  no operation moved by 1% of the time
where the time goes in v4:
time: 172 us; the launch traced here: 171 us
  Pallas kernels  169 us (98%)
  local copies, waits for them, and re-layouts  2.46 us (1%)
    pallas_call x1, Pallas kernels, moe(): pl.pallas_call(functools.partial(moe_kernel, group, experts, capacity, lo...  169 us

profile of v4, /device:TPU:0, one launch (start us, length us, event | category | flops | bytes accessed | tf_op | source)
XLA Modules:
  0.0 171.4 jit_solution(17525976552890197291)
XLA Ops:
  0.0 168.9 %moe.1 = bf16[256,2560]{1,0:T(8,128)(2,1)} custom-call(bf16[256,2560]{1,0:T(8,128)(2,1)} %x_hbm.1, s32[6,256]{1,0:T(8,128)} %bitcast.5, bf16[2560]{0:T(1024)(128)(2,1)} %gain_ref.1, bf16[64,2560]{1,0:T(8,128)(2,1)} %bitcast.3, bf16[1,2560]{1,0:T(2,128)(2,1)} %bitcast.4, bf16[2560,3072]{1,0:T(8,128)(2,1)} %sg_hbm.1, bf16[2560,3072]{1,0:T(8,128)(2,1)} %su_hbm.1, ...), custom_call_target="tpu_custom_call" | custom-call | flops 72477573120 | bytes 377487360 | tf_op jit(solution)/shard_map/moe/pallas_call | solution.py:482
  168.9 2.5 %copy.13 = bf16[256,2560]{1,0:T(8,128)(2,1)} copy(bf16[256,2560]{1,0:T(8,128)(2,1)} %moe.1) | data formatting | bytes 2621440
